TPU v7x, 128 devices: a whole 4x4x4 slice. The times are simulated.
128 devices in a mesh: seq: 16 (over z_hi, y, core), head: 8 (over x, z_lo).
Axes of the slice: x: 4, y: 4, z: 4 (z_hi: 2, z_lo: 2; z = z_hi * 2 + z_lo), core: 2. Of those that a mesh axis runs over, the one named last changes fastest.
Arguments:
- latent: bfloat16 [16, 1024, 2048], P('seq', None, 'head'), may hold values from -6 to 6
- modulation: float32 [9, 2048], replicated, may hold values from -3 to 3
- spatial_qkv: bfloat16 [3, 2048, 2048], P(None, None, 'head')
- spatial_out: bfloat16 [2048, 2048], P('head'), may hold values from -0.125 to 0.125
- temporal_qkv: bfloat16 [3, 2048, 2048], P(None, None, 'head')
- temporal_out: bfloat16 [2048, 2048], P('head'), may hold values from -0.125 to 0.125
- hidden_weight: bfloat16 [2048, 8192], P(None, 'head'), may hold values from -0.125 to 0.125
- output_weight: bfloat16 [8192, 2048], P('head'), may hold values from -0.0625 to 0.0625
Outputs:
- block_out: bfloat16 [16, 1024, 2048], P(None, 'seq', 'head')
All inputs are finite; a program needn't handle non-finite values.
Results may differ from a plain program's by a relative error of at most 0.009.
Values may be sent and summed in bfloat16 or wider, within the bound.
A program may use at most 128 MiB of HBM per device.

v0:
```python
import jax
import jax.numpy as jnp
from jax import lax
from jax.sharding import PartitionSpec as P

HD = 64


def split_up(shard, dim, devices):
    lengths = shard.shape
    blocks = shard.reshape(*lengths[:dim], devices, lengths[dim] // devices, *lengths[dim + 1 :])
    return jnp.moveaxis(blocks, dim, 0)


def sum_at_owner(shard, axis, dim):
    devices = lax.axis_size(axis)
    blocks = lax.all_to_all(split_up(shard, dim, devices), axis, 0, 0, tiled=True)
    return jnp.sum(blocks.astype(jnp.float32), axis=0)


def layer_norm(values):
    average = jnp.mean(values, axis=-1, keepdims=True)
    centred = values - average
    variance = jnp.mean(centred * centred, axis=-1, keepdims=True)
    return centred * lax.rsqrt(variance + 1e-06)


def modulate(stream, modulation, offset):
    normed = layer_norm(stream.astype(jnp.float32))
    return (normed * (1.0 + modulation[offset + 1]) + modulation[offset]).astype(jnp.bfloat16)


def attend(query, keys, values):
    scores = jnp.einsum(
        "glhd,gmhd->ghlm", query, keys, preferred_element_type=jnp.float32
    ) * HD ** (-0.5)
    attn_weights = jax.nn.softmax(scores, axis=-1).astype(jnp.bfloat16)
    return jnp.einsum(
        "ghlm,gmhd->glhd", attn_weights, values, preferred_element_type=jnp.float32
    ).astype(jnp.bfloat16)


def project_three(normed, weights):
    return [
        jnp.dot(normed, weights[member], preferred_element_type=jnp.float32).astype(jnp.bfloat16)
        for member in range(3)
    ]


def column_adder(columns, portion):
    return jnp.dot(portion, columns, preferred_element_type=jnp.float32)


def per_device(
    latent,
    modulation,
    spatial_qkv,
    spatial_out,
    temporal_qkv,
    temporal_out,
    hidden_weight,
    output_weight,
):
    width_local = latent.shape[2]
    heads_local = width_local // HD
    anchor = lax.axis_index("head") * width_local
    local_rows = lax.dynamic_slice_in_dim(modulation, anchor, width_local, 1)
    full_spatial = lax.all_gather(latent, "head", axis=2, tiled=True)
    normed = modulate(full_spatial, modulation, 0)
    frames_local = latent.shape[0]
    patches = latent.shape[1]
    query, keys, values = [
        member.reshape(frames_local, patches, heads_local, HD)
        for member in project_three(normed, spatial_qkv)
    ]
    spatial = lax.map(
        lambda triple: attend(triple[0][None], triple[1][None], triple[2][None])[0],
        (query, keys, values),
    )
    spatial = spatial.reshape(frames_local, patches, width_local)
    columns = lax.all_to_all(spatial_out, "head", split_axis=1, concat_axis=0, tiled=True)
    reduced = column_adder(columns, lax.all_gather(spatial, "head", axis=2, tiled=True))
    stream_one = (latent.astype(jnp.float32) + local_rows[2] * reduced).astype(jnp.bfloat16)
    stream_temporal = lax.all_to_all(stream_one, "seq", split_axis=1, concat_axis=0, tiled=True)
    full_temporal = lax.all_gather(stream_temporal, "head", axis=2, tiled=True)
    normed = modulate(full_temporal, modulation, 3)
    query, keys, values = project_three(normed, temporal_qkv)
    frames = stream_temporal.shape[0]
    patches_local = stream_temporal.shape[1]

    def to_groups(tensor):
        return jnp.transpose(tensor.reshape(frames, patches_local, heads_local, HD), (1, 0, 2, 3))

    temporal = attend(to_groups(query), to_groups(keys), to_groups(values))
    temporal = jnp.transpose(temporal, (1, 0, 2, 3)).reshape(frames, patches_local, width_local)
    columns = lax.all_to_all(temporal_out, "head", split_axis=1, concat_axis=0, tiled=True)
    reduced = column_adder(columns, lax.all_gather(temporal, "head", axis=2, tiled=True))
    stream_two = (stream_temporal.astype(jnp.float32) + local_rows[5] * reduced).astype(
        jnp.bfloat16
    )
    full_two = lax.all_gather(stream_two, "head", axis=2, tiled=True)
    normed = modulate(full_two, modulation, 6)
    pre_act = jnp.dot(normed, hidden_weight, preferred_element_type=jnp.float32)
    hidden = jax.nn.gelu(pre_act, approximate=True).astype(jnp.bfloat16)
    partial_sums = jnp.dot(hidden, output_weight, preferred_element_type=jnp.float32)
    reduced = sum_at_owner(partial_sums.astype(jnp.bfloat16), "head", 2)
    return (stream_two.astype(jnp.float32) + local_rows[8] * reduced).astype(jnp.bfloat16)


def solution(mesh):
    in_specs = (
        P("seq", None, "head"),
        P(),
        P(None, None, "head"),
        P("head", None),
        P(None, None, "head"),
        P("head", None),
        P(None, "head"),
        P("head", None),
    )
    out_specs = P(None, "seq", "head")
    return jax.shard_map(
        per_device, mesh=mesh, in_specs=in_specs, out_specs=out_specs, check_vma=False
    )
```

profile of v0, /device:TPU:8, one launch (start us, length us, event | category | flops | bytes accessed | tf_op | source)
XLA Modules:
  0.0 685.8 jit_solution(7628114898617417352)
XLA Ops:
  8.4 99.1 %all-gather.6.cloned.1.call-done = bf16[1,1024,2048]{2,1,0:T(8,128)(2,1)} async-done(((bf16[1,1024,256]{2,1,0:T(8,128)(2,1)}), bf16[1,1024,2048]{2,1,0:T(8,128)(2,1)}) %all-gather.6.cloned.1.call-update) | async-done | bytes 4194320 | tf_op jit(solution)/shard_map/all_gather | solution.py:68
  107.6 3.0 convert_reduce_fusion.2
  118.1 5.2 fusion.130
  123.3 8.1 %fusion.136 = f32[4,1024,1024]{1,2,0:T(8,128)} fusion(bf16[1024,4,64]{0,2,1:T(8,128)(2,1)S(1)} %bitcast.142, bf16[1024,4,64]{0,2,1:T(8,128)(2,1)S(1)} %bitcast.144), kind=kOutput, calls=%fused_computation.124 | convolution fusion | flops 536870912 | bytes 17825792 | tf_op jit(solution)/shard_map/while/body/eval_jaxpr/glhd,gmhd->ghlm/dot_general | solution.py:34
  131.4 16.0 %fusion.69 = bf16[4,64,1024]{2,1,0:T(8,128)(2,1)} fusion(bf16[1024,4,64]{0,2,1:T(8,128)(2,1)S(1)} %bitcast.162, f32[4,1024]{1,0:T(4,128)S(1)} %fusion.130, f32[4,1024,1024]{1,2,0:T(8,128)} %fusion.136), kind=kOutput, calls=%fused_computation.78 | convolution fusion | flops 558109696 | bytes 17842176 | tf_op jit(solution)/shard_map/while/body/eval_jaxpr/ghlm,gmhd->glhd/dot_general | solution.py:38
  148.7 6.0 all-to-all-start
  155.6 21.3 %all-to-all-done = bf16[256,8,256]{0,2,1:T(8,128)(2,1)S(1)} async-done(((bf16[256,8,256]{0,2,1:T(8,128)(2,1)}), bf16[256,8,256]{0,2,1:T(8,128)(2,1)S(1)}, u32[]{:S(2)}, u32[]{:S(2)}) %all-to-all-start) | async-done | bytes 1048608 | tf_op jit(solution)/shard_map/all_to_all | solution.py:81
  177.5 71.1 %all-gather.8.cloned.1.call-done = bf16[1,1024,2048]{1,2,0:T(8,128)(2,1)} async-done(((bf16[1,1024,256]{1,2,0:T(8,128)(2,1)}), bf16[1,1024,2048]{1,2,0:T(8,128)(2,1)}) %all-gather.8.cloned.1.call-update) | async-done | bytes 4194320 | tf_op jit(solution)/shard_map/all_gather | solution.py:82
  248.6 3.5 fusion.65
  253.4 3.8 reduce.6
  257.4 15.9 %all_to_all.55 = bf16[16,2,8192]{2,1,0:T(2,128)(2,1)S(1)} all-to-all(bf16[16,2,8192]{2,1,0:T(2,128)(2,1)S(1)} %reshape.181), channel_id=1, replica_groups=mesh['seq'=16,'head'=8] {'seq'}, dimensions={0} | all-to-all | bytes 1048576 | tf_op jit(solution)/shard_map/all_to_all | solution.py:84
  274.9 94.6 %all-gather.10.cloned.1.call-done = bf16[16,64,2048]{2,1,0:T(8,128)(2,1)} async-done(((bf16[16,64,256]{2,1,0:T(8,128)(2,1)}), bf16[16,64,2048]{2,1,0:T(8,128)(2,1)}) %all-gather.10.cloned.1.call-update) | async-done | bytes 4194320 | tf_op jit(solution)/shard_map/all_gather | solution.py:85
  369.5 3.0 convert_reduce_fusion.1
  374.2 3.0 convolution_convert_fusion.1
  377.5 4.2 convolution_convert_fusion.2
  382.2 5.0 convolution_convert_fusion.3
  389.4 3.3 fusion.131
  397.4 24.8 %all_to_all.56 = bf16[256,8,256]{2,0,1:T(8,128)(2,1)S(1)} all-to-all(bf16[256,8,256]{2,0,1:T(8,128)(2,1)S(1)} %bitcast.138), channel_id=1, replica_groups=mesh['seq'=16,'head'=8] {'head'}, dimensions={1} | all-to-all | bytes 2097152 | tf_op jit(solution)/shard_map/all_to_all | solution.py:96
  422.2 74.8 %all-gather.12.cloned.1.call-done = bf16[16,64,2048]{2,1,0:T(8,128)(2,1)} async-done(((bf16[16,64,256]{2,1,0:T(8,128)(2,1)}), bf16[16,64,2048]{2,1,0:T(8,128)(2,1)}) %all-gather.12.cloned.1.call-update) | async-done | bytes 4194320 | tf_op jit(solution)/shard_map/all_gather | solution.py:97
  497.0 4.2 fusion.68
  501.3 100.4 %all-gather.14.cloned.1.call-done = bf16[16,64,2048]{2,1,0:T(8,128)(2,1)} async-done(((bf16[16,64,256]{2,1,0:T(8,128)(2,1)}), bf16[16,64,2048]{2,1,0:T(8,128)(2,1)}) %all-gather.14.cloned.1.call-update) | async-done | bytes 4194320 | tf_op jit(solution)/shard_map/all_gather | solution.py:101
  601.7 3.0 convert_reduce_fusion
  606.4 15.3 %fusion.45 = bf16[16,64,2048]{2,1,0:T(8,128)(2,1)} fusion(bf16[1024,2048]{1,0:T(8,128)(2,1)} %param.15, bf16[16,64,2048]{2,1,0:T(8,128)(2,1)} %all-gather.14.cloned.1.call-done, bf16[2048,1024]{1,0:T(8,128)(2,1)} %param.14, f32[2048]{0:T(1024)S(1)} %bitcast.152, f32[2048]{0:T(1024)S(1)} %bitcast.151, f32[16,64]{1,0:T(8,128)S(1)} %add_rsqrt_fusion, ...), kind=kOutput, calls=%fused_computation.54 | convolution fusion | flops 8614051840 | bytes 16801792 | tf_op jit(solution)/shard_map/dot_general | solution.py:105
  624.5 52.6 %all_to_all.57 = bf16[8,16,64,256]{3,2,1,0:T(8,128)(2,1)S(1)} all-to-all(bf16[8,16,64,256]{3,2,1,0:T(8,128)(2,1)S(1)} %bitcast.133), channel_id=1, replica_groups=mesh['seq'=16,'head'=8] {'head'}, dimensions={0} | all-to-all | bytes 8388608 | tf_op jit(solution)/shard_map/all_to_all | solution.py:17
  (60 shorter events, 31.0 us)
Async XLA Ops:
  6.5 101.0 %all-gather.6.cloned.1.call-start = ((), (), s32[]{:S(2)}) async-start(), calls=%async_computation.4 | async-start | bytes 4718592 | tf_op jit(solution)/shard_map/all_gather | solution.py:68
  7.3 241.3 %all-gather.8.cloned.1.call-start = ((), (), s32[]{:S(2)}) async-start(), calls=%async_computation.5 | async-start | bytes 4718592 | tf_op jit(solution)/shard_map/all_gather | solution.py:82
  107.6 3.4 copy-start
  112.3 1.9 copy-start.8
  131.4 16.0 %copy-start.5 = (bf16[256,2048]{1,0:T(8,128)(2,1)S(1)}, bf16[256,2048]{1,0:T(8,128)(2,1)}, u32[]{:S(2)}) copy-start(bf16[256,2048]{1,0:T(8,128)(2,1)} %param.11) | copy-start | bytes 3145732
  147.4 101.2 %copy-start.7 = (bf16[1,1024,256]{2,1,0:T(8,128)(2,1)S(1)}, bf16[1,1024,256]{2,1,0:T(8,128)(2,1)}, u32[]{:S(2)}) copy-start(bf16[1,1024,256]{2,1,0:T(8,128)(2,1)} %param.8) | copy-start | bytes 1572868
  148.7 28.2 %all-to-all-start = ((bf16[256,8,256]{0,2,1:T(8,128)(2,1)}), bf16[256,8,256]{0,2,1:T(8,128)(2,1)S(1)}, u32[]{:S(2)}, u32[]{:S(2)}) async-start(bf16[256,8,256]{0,2,1:T(8,128)(2,1)} %bitcast.14), calls=%async_computation | async-start | bytes 2097152 | tf_op jit(solution)/shard_map/all_to_all | solution.py:81
  154.7 214.7 %all-gather.10.cloned.1.call-start = ((), (), s32[]{:S(2)}) async-start(), calls=%async_computation.6 | async-start | bytes 4718592 | tf_op jit(solution)/shard_map/all_gather | solution.py:85
  274.7 222.4 %all-gather.12.cloned.1.call-start = ((), (), s32[]{:S(2)}) async-start(), calls=%async_computation.7 | async-start | bytes 4718592 | tf_op jit(solution)/shard_map/all_gather | solution.py:97
  369.5 3.4 copy-start.1
  395.2 2.1 copy-start.6
  395.2 101.8 %copy-start.3 = (bf16[1,1024,256]{2,1,0:T(8,128)(2,1)S(1)}, bf16[1,1024,256]{2,1,0:T(8,128)(2,1)}, u32[]{:S(2)}) copy-start(bf16[1,1024,256]{2,1,0:T(8,128)(2,1)} %copy.55) | copy-start | bytes 1572868
  397.2 204.5 %all-gather.14.cloned.1.call-start = ((), (), s32[]{:S(2)}) async-start(), calls=%async_computation.8 | async-start | bytes 4718592 | tf_op jit(solution)/shard_map/all_gather | solution.py:101
  601.7 3.4 copy-start.2
  677.1 1.0 copy-start.4
Sparse Core Ops, SparseCore 0:
  8.9 98.6 all-gather.5
  147.5 101.0 all-gather.7
  274.8 94.6 all-gather.9
  397.3 99.6 all-gather.11
  501.4 100.2 all-gather.13
where the time goes:
time: 696 us; the launch traced here: 686 us
  waiting for transfers between devices  462 us (66%)
  blocking collectives  93.3 us (13%)
  matrix products  74.2 us (11%)
  other arithmetic  21.1 us (3%)
  local copies, waits for them, and re-layouts  15.2 us (2%)
  between operations  13.6 us (2%)
    all_gather x1, waiting for transfers between devices, per_device(): full_two = lax.all_gather(stream_two, 'head', axis=2, tiled=True)  100 us
    all_gather x1, waiting for transfers between devices, per_device(): full_spatial = lax.all_gather(latent, 'head', axis=2, tiled=True)  99.1 us
    all_gather x1, waiting for transfers between devices, per_device(): full_temporal = lax.all_gather(stream_temporal, 'head', axis=2, tiled=True)  94.6 us
    all_gather x1, waiting for transfers between devices, per_device(): lax.all_gather(temporal, 'head', axis=2, tiled=True)  74.8 us
    all_gather x1, waiting for transfers between devices, per_device(): lax.all_gather(spatial, 'head', axis=2, tiled=True)  71.1 us
    all_to_all x1, blocking collectives, sum_at_owner(): lax.all_to_all(split_up(shard, dim, devices), axis, 0, 0, tiled=True)  52.6 us
    all_to_all x1, blocking collectives, per_device(): lax.all_to_all(temporal_out, 'head', split_axis=1, concat_axis=0, tiled=T...  24.8 us
    all_to_all x1, waiting for transfers between devices, per_device(): lax.all_to_all(spatial_out, 'head', split_axis=1, concat_axis=0, tiled=True)  21.3 us
  transfers between devices with their start and end apart: 6, of which 6 were waited for; matrix products, arithmetic and copies ran while one was open for 1% of the time, Pallas kernels for 0%

commit v1 on v0

--- a/solution.py
+++ b/solution.py
@@ -1,9 +1,20 @@
+import functools
 import jax
 import jax.numpy as jnp
 from jax import lax
 from jax.sharding import PartitionSpec as P
 
 HD = 64
+
+
+def meet_the_quarters(w_in, ax_name):
+    inbox = []
+    for _ in range(lax.axis_size(ax_name)):
+        inbox.append(w_in)
+    return jnp.concatenate(lax.all_to_all(jnp.stack(inbox), ax_name, 0, 0), 2)
+
+
+wait_shards = functools.partial(meet_the_quarters, ax_name="head")
 
 
 def split_up(shard, dim, devices):
@@ -79,7 +90,7 @@
     )
     spatial = spatial.reshape(frames_local, patches, width_local)
     columns = lax.all_to_all(spatial_out, "head", split_axis=1, concat_axis=0, tiled=True)
-    reduced = column_adder(columns, lax.all_gather(spatial, "head", axis=2, tiled=True))
+    reduced = column_adder(columns, wait_shards(spatial))
     stream_one = (latent.astype(jnp.float32) + local_rows[2] * reduced).astype(jnp.bfloat16)
     stream_temporal = lax.all_to_all(stream_one, "seq", split_axis=1, concat_axis=0, tiled=True)
     full_temporal = lax.all_gather(stream_temporal, "head", axis=2, tiled=True)

time: 696 us -> 666 us (0.957)
  waiting for transfers between devices: 462 us -> 424 us
    all_gather x1 -> x0, waiting for transfers between devices: 71.1 us -> none  [per_device(): lax.all_gather(spatial, 'head', axis=2, tiled=True)]
    all_to_all x0 -> x1, waiting for transfers between devices: none -> 56.4 us  [meet_the_quarters(): return jnp.concatenate(lax.all_to_all(jnp.stack(inbox), ax_name, 0, 0), 2)]
    all_to_all x1, waiting for transfers between devices: 21.3 us -> 0.01 us  [per_device(): lax.all_to_all(spatial_out, 'head', split_axis=1, concat_axis=0, tiled=True)]
  transfers between devices with their start and end apart: 6 -> 6, of which waited for: 6 -> 5; matrix products, arithmetic and copies ran while one was open for 1% -> 7% of each run, Pallas kernels for 0% -> 0%
where the time goes in v1:
time: 666 us; the launch traced here: 657 us
  waiting for transfers between devices  424 us (64%)
  blocking collectives  93.8 us (14%)
  matrix products  73.9 us (11%)
  other arithmetic  21.1 us (3%)
  local copies, waits for them, and re-layouts  18.6 us (3%)
  between operations  13.6 us (2%)
  starting transfers between devices  11.6 us (2%)
    all_gather x1, waiting for transfers between devices, per_device(): full_two = lax.all_gather(stream_two, 'head', axis=2, tiled=True)  100 us
    all_gather x1, waiting for transfers between devices, per_device(): full_spatial = lax.all_gather(latent, 'head', axis=2, tiled=True)  97.8 us
    all_gather x1, waiting for transfers between devices, per_device(): full_temporal = lax.all_gather(stream_temporal, 'head', axis=2, tiled=True)  93.7 us
    all_gather x1, waiting for transfers between devices, per_device(): lax.all_gather(temporal, 'head', axis=2, tiled=True)  74.8 us
    all_to_all x1, waiting for transfers between devices, meet_the_quarters(): return jnp.concatenate(lax.all_to_all(jnp.stack(inbox), ax_name, 0, 0), 2)  56.4 us
    all_to_all x1, blocking collectives, sum_at_owner(): lax.all_to_all(split_up(shard, dim, devices), axis, 0, 0, tiled=True)  52.6 us
    all_to_all x1, blocking collectives, per_device(): lax.all_to_all(temporal_out, 'head', split_axis=1, concat_axis=0, tiled=T...  24.9 us
    dot_general x2, matrix products, attend(): jnp.einsum('ghlm,gmhd->glhd', attn_weights, values, preferred_element_typ...  18.2 us
  transfers between devices with their start and end apart: 6, of which 5 were waited for; matrix products, arithmetic and copies ran while one was open for 7% of the time, Pallas kernels for 0%

profile of v1, /device:TPU:8, one launch (start us, length us, event | category | flops | bytes accessed | tf_op | source)
XLA Modules:
  0.0 656.7 jit_solution(10458745117441268103)
XLA Ops:
  9.5 5.7 all-to-all-start.1
  16.3 97.8 %all-gather.5.cloned.1.call-done = bf16[1,1024,2048]{2,1,0:T(8,128)(2,1)} async-done(((bf16[1,1024,256]{2,1,0:T(8,128)(2,1)}), bf16[1,1024,2048]{2,1,0:T(8,128)(2,1)}) %all-gather.5.cloned.1.call-update) | async-done | bytes 4194320 | tf_op jit(solution)/shard_map/all_gather | solution.py:79
  114.2 3.0 convert_reduce_fusion.2
  124.7 5.2 fusion.119
  129.9 8.1 %fusion.125 = f32[4,1024,1024]{1,2,0:T(8,128)} fusion(bf16[1024,4,64]{0,2,1:T(8,128)(2,1)S(1)} %bitcast.137, bf16[1024,4,64]{0,2,1:T(8,128)(2,1)S(1)} %bitcast.139), kind=kOutput, calls=%fused_computation.122 | convolution fusion | flops 536870912 | bytes 17825792 | tf_op jit(solution)/shard_map/while/body/eval_jaxpr/glhd,gmhd->ghlm/dot_general | solution.py:45
  138.0 15.7 %fusion.58 = bf16[4,64,1024]{2,1,0:T(8,128)(2,1)S(1)} fusion(bf16[1024,4,64]{0,2,1:T(8,128)(2,1)S(1)} %bitcast.157, f32[4,1024]{1,0:T(4,128)S(1)} %fusion.119, f32[4,1024,1024]{1,2,0:T(8,128)} %fusion.125), kind=kOutput, calls=%fused_computation.76 | convolution fusion | flops 558109696 | bytes 17842176 | tf_op jit(solution)/shard_map/while/body/eval_jaxpr/ghlm,gmhd->glhd/dot_general | solution.py:49
  156.2 5.7 all-to-all-start
  163.4 56.4 %all-to-all-done = bf16[8,1,1024,256]{2,3,1,0:T(8,128)(2,1)} async-done(((bf16[8,1,1024,256]{2,3,1,0:T(8,128)(2,1)}), bf16[8,1,1024,256]{2,3,1,0:T(8,128)(2,1)}, u32[]{:S(2)}, u32[]{:S(2)}) %all-to-all-start) | async-done | bytes 4194336 | tf_op jit(solution)/shard_map/all_to_all | solution.py:14
  219.8 3.5 fusion.57
  224.6 3.8 reduce.6
  228.6 16.4 %all_to_all.60 = bf16[16,2,8192]{2,1,0:T(2,128)(2,1)S(1)} all-to-all(bf16[16,2,8192]{2,1,0:T(2,128)(2,1)S(1)} %reshape.187), channel_id=1, replica_groups=mesh['seq'=16,'head'=8] {'seq'}, dimensions={0} | all-to-all | bytes 1048576 | tf_op jit(solution)/shard_map/all_to_all | solution.py:95
  246.6 93.7 %all-gather.7.cloned.1.call-done = bf16[16,64,2048]{2,1,0:T(8,128)(2,1)} async-done(((bf16[16,64,256]{2,1,0:T(8,128)(2,1)}), bf16[16,64,2048]{2,1,0:T(8,128)(2,1)}) %all-gather.7.cloned.1.call-update) | async-done | bytes 4194320 | tf_op jit(solution)/shard_map/all_gather | solution.py:96
  340.4 3.0 convert_reduce_fusion.1
  345.0 3.0 convolution_convert_fusion.1
  348.4 4.2 convolution_convert_fusion.2
  353.1 5.0 convolution_convert_fusion.3
  360.3 3.3 fusion.120
  368.2 24.9 %all_to_all.61 = bf16[256,8,256]{2,0,1:T(8,128)(2,1)S(1)} all-to-all(bf16[256,8,256]{2,0,1:T(8,128)(2,1)S(1)} %bitcast.133), channel_id=1, replica_groups=mesh['seq'=16,'head'=8] {'head'}, dimensions={1} | all-to-all | bytes 2097152 | tf_op jit(solution)/shard_map/all_to_all | solution.py:107
  393.1 74.8 %all-gather.9.cloned.1.call-done = bf16[16,64,2048]{2,1,0:T(8,128)(2,1)} async-done(((bf16[16,64,256]{2,1,0:T(8,128)(2,1)}), bf16[16,64,2048]{2,1,0:T(8,128)(2,1)}) %all-gather.9.cloned.1.call-update) | async-done | bytes 4194320 | tf_op jit(solution)/shard_map/all_gather | solution.py:108
  467.9 4.2 fusion.56
  472.2 100.4 %all-gather.11.cloned.1.call-done = bf16[16,64,2048]{2,1,0:T(8,128)(2,1)} async-done(((bf16[16,64,256]{2,1,0:T(8,128)(2,1)}), bf16[16,64,2048]{2,1,0:T(8,128)(2,1)}) %all-gather.11.cloned.1.call-update) | async-done | bytes 4194320 | tf_op jit(solution)/shard_map/all_gather | solution.py:112
  572.6 3.0 convert_reduce_fusion
  577.3 15.3 %fusion.43 = bf16[16,64,2048]{2,1,0:T(8,128)(2,1)} fusion(bf16[1024,2048]{1,0:T(8,128)(2,1)} %param.15, bf16[16,64,2048]{2,1,0:T(8,128)(2,1)} %all-gather.11.cloned.1.call-done, bf16[2048,1024]{1,0:T(8,128)(2,1)} %param.14, f32[2048]{0:T(1024)S(1)} %bitcast.147, f32[2048]{0:T(1024)S(1)} %bitcast.146, f32[16,64]{1,0:T(8,128)S(1)} %add_rsqrt_fusion, ...), kind=kOutput, calls=%fused_computation.52 | convolution fusion | flops 8614051840 | bytes 16801792 | tf_op jit(solution)/shard_map/dot_general | solution.py:116
  595.4 52.6 %all_to_all.62 = bf16[8,16,64,256]{3,2,1,0:T(8,128)(2,1)S(1)} all-to-all(bf16[8,16,64,256]{3,2,1,0:T(8,128)(2,1)S(1)} %bitcast.128), channel_id=1, replica_groups=mesh['seq'=16,'head'=8] {'head'}, dimensions={0} | all-to-all | bytes 8388608 | tf_op jit(solution)/shard_map/all_to_all | solution.py:28
  (58 shorter events, 34.4 us)
Async XLA Ops:
  6.5 107.6 %all-gather.5.cloned.1.call-start = ((), (), s32[]{:S(2)}) async-start(), calls=%async_computation.5 | async-start | bytes 4718592 | tf_op jit(solution)/shard_map/all_gather | solution.py:79
  9.5 144.2 %all-to-all-start.1 = ((bf16[256,8,256]{0,2,1:T(8,128)(2,1)}), bf16[256,8,256]{0,2,1:T(8,128)(2,1)S(1)}, u32[]{:S(2)}, u32[]{:S(2)}) async-start(bf16[256,8,256]{0,2,1:T(8,128)(2,1)} %bitcast.16), calls=%async_computation.1 | async-start | bytes 2097152 | tf_op jit(solution)/shard_map/all_to_all | solution.py:92
  114.2 3.4 copy-start
  118.9 1.9 copy-start.7
  156.2 63.6 %copy-start.6 = (bf16[1,1024,256]{2,1,0:T(8,128)(2,1)S(1)}, bf16[1,1024,256]{2,1,0:T(8,128)(2,1)}, u32[]{:S(2)}) copy-start(bf16[1,1024,256]{2,1,0:T(8,128)(2,1)} %param.8) | copy-start | bytes 1572868
  156.2 63.6 %all-to-all-start = ((bf16[8,1,1024,256]{2,3,1,0:T(8,128)(2,1)}), bf16[8,1,1024,256]{2,3,1,0:T(8,128)(2,1)}, u32[]{:S(2)}, u32[]{:S(2)}) async-start(bf16[8,1,1024,256]{2,3,1,0:T(8,128)(2,1)} %stack.3), calls=%async_computation | async-start | bytes 8388608 | tf_op jit(solution)/shard_map/all_to_all | solution.py:14
  161.9 178.4 %all-gather.7.cloned.1.call-start = ((), (), s32[]{:S(2)}) async-start(), calls=%async_computation.6 | async-start | bytes 4718592 | tf_op jit(solution)/shard_map/all_gather | solution.py:96
  246.4 221.5 %all-gather.9.cloned.1.call-start = ((), (), s32[]{:S(2)}) async-start(), calls=%async_computation.7 | async-start | bytes 4718592 | tf_op jit(solution)/shard_map/all_gather | solution.py:108
  340.4 3.4 copy-start.1
  366.1 2.1 copy-start.5
  366.1 101.8 %copy-start.3 = (bf16[1,1024,256]{2,1,0:T(8,128)(2,1)S(1)}, bf16[1,1024,256]{2,1,0:T(8,128)(2,1)}, u32[]{:S(2)}) copy-start(bf16[1,1024,256]{2,1,0:T(8,128)(2,1)} %copy.58) | copy-start | bytes 1572868
  368.1 204.5 %all-gather.11.cloned.1.call-start = ((), (), s32[]{:S(2)}) async-start(), calls=%async_computation.8 | async-start | bytes 4718592 | tf_op jit(solution)/shard_map/all_gather | solution.py:112
  572.6 3.4 copy-start.2
  647.9 1.0 copy-start.4
Sparse Core Ops, SparseCore 0:
  8.9 105.2 all-gather.4
  246.5 93.7 all-gather.6
  368.2 99.6 all-gather.8
  472.3 100.2 all-gather.10
